TPU v7x, 32 devices: a whole 2x2x4 slice. The times are simulated.
32 devices in a mesh: dp: 8 (over y, x, core), fsdp: 4 (over z).
Axes of the slice: x: 2, y: 2, z: 4, core: 2. Of those that a mesh axis runs over, the one named last changes fastest.
Arguments:
- hidden: bfloat16 [16384, 8192], P('dp', 'fsdp'), may hold values from -50 to 50
- logit_grad: bfloat16 [16384, 256], P('dp'), may hold values from -20 to 20
- master: float32 [256, 8192], P('dp', 'fsdp'), may hold values from -6 to 6
- moment_one: float32 [256, 8192], P('dp', 'fsdp'), may hold values from -4 to 4
- moment_two: float32 [256, 8192], P('dp', 'fsdp'), may hold values from 0.25 to 4
Outputs:
- new_rows: bfloat16 [256, 8192], P(None, 'fsdp')
- new_master: float32 [256, 8192], P('dp', 'fsdp')
- new_one: float32 [256, 8192], P('dp', 'fsdp')
- new_two: float32 [256, 8192], P('dp', 'fsdp')
All inputs are finite; a program needn't handle non-finite values.
Results may differ from a plain program's by a relative error of at most 0.012.
Values may be sent and summed in bfloat16 or wider, within the bound.
A program may use at most 64 MiB of HBM per device.

v0:
```python
import functools

import jax
import jax.numpy as jnp
from jax import lax
from jax.experimental import pallas as pl
from jax.experimental.pallas import tpu as pltpu
from jax.sharding import PartitionSpec as P

MESH = pl.DeviceIdType.MESH
LOAD_CHUNKS = 4
GATHER_CHUNKS = 2
VMEM_BYTES = 67_043_328


def pieces(width, wanted):
    count = wanted
    while count > 1 and width % (count * 128):
        count -= 1
    return count


def kernel(
    n, depth, chunks, gathers,
    hid, lgr, mas, one, two,
    rows_out, mas_out, one_out, two_out,
    lgr_v, lgt_v, hid_v, mas_v, one_v, two_v,
    stage, paired, sums, arrived, grad, sq_all,
    hid_sem, lgr_sem, state_sem, pair_send, pair_recv, chip_send, chip_recv,
    sq_send, sq_recv, ag_send, ag_recv, relay_send, relay_recv,
):
    chips = n // 2
    total = n * depth
    rows, width = grad.shape
    dp, fs = lax.axis_index("dp"), lax.axis_index("fsdp")
    chip, core = dp // 2, dp % 2
    other = 1 - core
    me = dp * depth + fs
    wc, wa = width // chunks, width // gathers

    lgr_copy = pltpu.make_async_copy(lgr, lgr_v, lgr_sem)
    lgr_copy.start()
    loads = []
    for j in range(chunks):
        load = pltpu.make_async_copy(hid.at[:, pl.ds(j * wc, wc)], hid_v.at[j], hid_sem.at[j])
        load.start()
        loads.append(load)
    states = []
    for i, (src, dst) in enumerate(((mas, mas_v), (one, one_v), (two, two_v))):
        load = pltpu.make_async_copy(src, dst, state_sem.at[i])
        load.start()
        states.append(load)

    def each_other_device(act):
        def visit(i):
            index = (me + i) % total
            act((index // depth, index % depth))

        if total <= 64:
            for i in range(1, total):
                visit(i)
        else:
            lax.fori_loop(1, total, lambda i, carry: (visit(i), carry)[1], 0)

    barrier = pltpu.get_barrier_semaphore()
    each_other_device(
        lambda to: pl.semaphore_signal(barrier, inc=1, device_id=to, device_id_type=MESH)
    )

    lgr_copy.wait()
    lgt_v[...] = lgr_v[...].T

    def remote(src, dst, send, recv, to):
        return pltpu.make_async_remote_copy(
            src_ref=src, dst_ref=dst, send_sem=send, recv_sem=recv, device_id=to, device_id_type=MESH
        )

    partner = (2 * chip + other, fs)
    others = [(chip + o) % chips for o in range(1, chips)]

    def pair_copy(j):
        return remote(stage.at[j, other], paired.at[j], pair_send.at[j], pair_recv.at[j], partner)

    def chip_copy(j, q, slot):
        return remote(
            sums.at[j, q], arrived.at[j, slot], chip_send.at[j, q], chip_recv.at[j, slot],
            (2 * q + core, fs),
        )

    def chip_sum(j):
        pair_copy(j).wait_recv()
        for q in others:
            both = stage[j, core, q].astype(jnp.float32) + paired[j, q].astype(jnp.float32)
            sums[j, q] = both.astype(jnp.bfloat16)
            chip_copy(j, q, chip).start()
        grad[:, pl.ds(j * wc, wc)] = stage[j, core, chip].astype(jnp.float32) + paired[
            j, chip
        ].astype(jnp.float32)

    for j in range(chunks):
        loads[j].wait()
        part = jnp.dot(lgt_v[...], hid_v[j], preferred_element_type=jnp.float32)
        part = part.astype(jnp.bfloat16)
        for q in range(chips):
            for c in range(2):
                d = 2 * q + c
                stage[j, c, q] = part[d * rows : (d + 1) * rows, :]
        if j == 0:
            pl.semaphore_wait(barrier, total - 1)
        pair_copy(j).start()
        if j > 0:
            chip_sum(j - 1)
    chip_sum(chunks - 1)

    squares = jnp.zeros((1, 128), jnp.float32)
    for j in range(chunks):
        span = pl.ds(j * wc, wc)
        value = grad[:, span]
        for q in others:
            chip_copy(j, q, q).wait_recv()
            value = value + arrived[j, q].astype(jnp.float32)
        grad[:, span] = value
        column = jnp.sum(value * value, axis=0, keepdims=True)
        for s in range(wc // 128):
            squares = squares + column[:, s * 128 : (s + 1) * 128]

    sq_all[me] = squares
    each_other_device(
        lambda to: remote(sq_all.at[me], sq_all.at[me], sq_send, sq_recv, to).start()
    )
    for load in states:
        load.wait()
    everyone = sq_all.at[pl.ds(0, total - 1)]
    pltpu.make_async_copy(everyone, everyone, sq_recv).wait()
    sumsq = jnp.sum(jnp.sum(sq_all[...], axis=0), axis=1, keepdims=True)
    rms = jnp.sqrt(sumsq / (rows * n * width * depth))
    factor = jnp.where(rms > 1.0, 1.0 / rms, 1.0)

    def cols(k):
        return pl.ds(k * wa, wa)

    def rows_of(d):
        return pl.ds(pl.multiple_of(d * rows, rows), rows)

    def gather_copy(k, d, to, send, recv):
        block = rows_out.at[rows_of(d), cols(k)]
        return remote(block, block, send, recv, to)

    def direct(k, source, q):
        return gather_copy(k, 2 * source + core, (2 * q + core, fs), ag_send.at[k, q], ag_recv.at[k, source])

    def relay(k, q, side):
        return gather_copy(k, 2 * q + side, partner, relay_send.at[k, q], relay_recv.at[k, q])

    for k in range(gathers):
        span = cols(k)
        clipped = factor * grad[:, span]
        new_one = 0.9 * one_v[:, span] + 0.1 * clipped
        new_two = 0.95 * two_v[:, span] + 0.05 * clipped * clipped
        first = new_one / (1.0 - 0.9**10)
        second = new_two / (1.0 - 0.95**10)
        held = mas_v[:, span]
        new_master = held - 0.05 * (first / (jnp.sqrt(second) + 1e-08) + 0.1 * held)
        rows_out[rows_of(dp), span] = new_master.astype(jnp.bfloat16)
        for q in others:
            direct(k, chip, q).start()
        relay(k, chip, core).start()
        one_out[:, span] = new_one
        two_out[:, span] = new_two
        mas_out[:, span] = new_master
    for k in range(gathers):
        for q in others:
            direct(k, q, q).wait_recv()
            relay(k, q, core).start()
    for k in range(gathers):
        for q in [chip] + others:
            relay(k, q, other).wait_recv()

    for j in range(chunks):
        pair_copy(j).wait_send()
        for q in others:
            chip_copy(j, q, chip).wait_send()
    pltpu.make_async_copy(everyone, everyone, sq_send).wait()
    for k in range(gathers):
        for q in others:
            direct(k, chip, q).wait_send()
            relay(k, q, core).wait_send()
        relay(k, chip, core).wait_send()


def write_out(*refs):
    sems = refs[8]
    copies = [pltpu.make_async_copy(refs[i], refs[4 + i], sems.at[i]) for i in range(4)]
    for copy in copies:
        copy.start()
    for copy in copies:
        copy.wait()


def shards(n, depth, hidden, logit_grad, master, moment_one, moment_two):
    tokens, width = hidden.shape
    slab = logit_grad.shape[1]
    rows = master.shape[0]
    chips = n // 2
    chunks = pieces(width, LOAD_CHUNKS)
    gathers = pieces(width, GATHER_CHUNKS)
    wc = width // chunks
    f32, bf16 = jnp.float32, jnp.bfloat16
    state = ((rows, width), f32)
    shapes = (((slab, width), bf16), state, state, state)
    kept = slab * width * 2 + 3 * rows * width * 4
    dma = pltpu.SemaphoreType.DMA
    anywhere = pl.BlockSpec(memory_space=pl.ANY)
    in_vmem = pl.BlockSpec(memory_space=pltpu.VMEM)
    held = pl.pallas_call(
        functools.partial(kernel, n, depth, chunks, gathers),
        out_shape=tuple(pltpu.VMEM(*shape) for shape in shapes),
        in_specs=[anywhere] * 5,
        out_specs=(in_vmem,) * 4,
        scratch_shapes=[
            pltpu.VMEM((tokens, slab), bf16),
            pltpu.VMEM((slab, tokens), bf16),
            pltpu.VMEM((chunks, tokens, wc), bf16),
            pltpu.VMEM((rows, width), f32),
            pltpu.VMEM((rows, width), f32),
            pltpu.VMEM((rows, width), f32),
            pltpu.VMEM((chunks, 2, chips, rows, wc), bf16),
            pltpu.VMEM((chunks, chips, rows, wc), bf16),
            pltpu.VMEM((chunks, chips, rows, wc), bf16),
            pltpu.VMEM((chunks, chips, rows, wc), bf16),
            pltpu.VMEM((rows, width), f32),
            pltpu.VMEM((n * depth, 1, 128), f32),
            dma((chunks,)),
            dma,
            dma((3,)),
            dma((chunks,)),
            dma((chunks,)),
            dma((chunks, chips)),
            dma((chunks, chips)),
            dma,
            dma,
            dma((gathers, chips)),
            dma((gathers, chips)),
            dma((gathers, chips)),
            dma((gathers, chips)),
        ],
        compiler_params=pltpu.CompilerParams(
            collective_id=0, has_side_effects=True, vmem_limit_bytes=VMEM_BYTES - kept - 96 * 1024
        ),
    )(hidden, logit_grad, master, moment_one, moment_two)
    return pl.pallas_call(
        write_out,
        out_shape=tuple(pltpu.HBM(*shape) for shape in shapes),
        in_specs=[anywhere] * 4,
        out_specs=(anywhere,) * 4,
        scratch_shapes=[dma((4,))],
        compiler_params=pltpu.CompilerParams(vmem_limit_bytes=1024 * 1024),
    )(*held)


def solution(mesh):
    placed = (P("dp", "fsdp"), P("dp", None), P("dp", "fsdp"), P("dp", "fsdp"), P("dp", "fsdp"))
    return jax.shard_map(
        functools.partial(shards, mesh.shape["dp"], mesh.shape["fsdp"]),
        mesh=mesh,
        in_specs=placed,
        out_specs=(P(None, "fsdp"), P("dp", "fsdp"), P("dp", "fsdp"), P("dp", "fsdp")),
        check_vma=False,
    )
```

profile of v0, /device:TPU:0, one launch (start us, length us, event | category | flops | bytes accessed | tf_op | source)
XLA Modules:
  0.0 33.1 jit_solution(9134755845285284766)
XLA Ops:
  0.6 31.2 %shard_map.84 = (bf16[256,2048]{1,0:T(8,128)(2,1)S(1)}, f32[32,2048]{1,0:T(8,128)S(1)}, f32[32,2048]{1,0:T(8,128)S(1)}, f32[32,2048]{1,0:T(8,128)S(1)}) custom-call(bf16[2048,2048]{1,0:T(8,128)(2,1)} %hid.1, bf16[2048,256]{1,0:T(8,128)(2,1)} %lgr.1, f32[32,2048]{1,0:T(8,128)} %mas.1, f32[32,2048]{1,0:T(8,128)} %one.1, f32[32,2048]{1,0:T(8,128)} %two.1), custom_call_target="tpu_custom_call" | custom-call | tf_op jit(solution)/shard_map/pallas_call | solution.py:215
  31.9 1.3 %shard_map.85 = (bf16[256,2048]{1,0:T(8,128)(2,1)}, f32[32,2048]{1,0:T(8,128)}, f32[32,2048]{1,0:T(8,128)}, f32[32,2048]{1,0:T(8,128)}) custom-call(bf16[256,2048]{1,0:T(8,128)(2,1)S(1)} %get-tuple-element.8.refs_0_, f32[32,2048]{1,0:T(8,128)S(1)} %get-tuple-element.9.refs_1_, f32[32,2048]{1,0:T(8,128)S(1)} %get-tuple-element.10.refs_2_, ...), custom_call_target="tpu_custom_call" | custom-call | tf_op jit(solution)/shard_map/pallas_call | solution.py:251
where the time goes:
time: 33.3 us; the launch traced here: 33.1 us
  Pallas kernels  32.5 us (98%)
  between operations  0.64 us (2%)
    pallas_call x1, Pallas kernels, shards(): pl.pallas_call(functools.partial(kernel, n, depth, chunks, gathers), out_...  31.2 us
    pallas_call x1, Pallas kernels, shards(): pl.pallas_call(write_out, out_shape=tuple((pltpu.HBM(*shape) for shape in...  1.26 us

commit v1 on v0

--- a/solution.py
+++ b/solution.py
@@ -11,6 +11,11 @@
 LOAD_CHUNKS = 4
 GATHER_CHUNKS = 2
 VMEM_BYTES = 67_043_328
+UNITS = 8
+PARTS = 4
+CHUNKS = ((1, False), (2, False), (2, False), (2, False), (1, False))
+PIECES = ((2, True), (2, False), (2, False), (2, False))
+AHEAD = 2
 
 
 def pieces(width, wanted):
@@ -20,7 +25,7 @@
     return count
 
 
-def kernel(
+def direct_kernel(
     n, depth, chunks, gathers,
     hid, lgr, mas, one, two,
     rows_out, mas_out, one_out, two_out,
@@ -188,6 +193,270 @@
         relay(k, chip, core).wait_send()
 
 
+def spans(width, plan):
+    unit, start, result = width // UNITS, 0, []
+    for count, relayed in plan:
+        result.append((start, count * unit, relayed))
+        start += count * unit
+    return result
+
+
+def square_scratch(n, depth, tokens, slab, rows, width):
+    f32, bf16 = jnp.float32, jnp.bfloat16
+    dma = pltpu.SemaphoreType.DMA
+    chunks = [(w, relayed) for _, w, relayed in spans(width, CHUNKS)]
+    state = pltpu.VMEM((rows, width), f32)
+    stage = tuple(pltpu.VMEM((2, n // 2, rows, w), bf16) for w, _ in chunks)
+    paired = tuple(pltpu.VMEM((n // 2, rows, w), bf16) for w, _ in chunks)
+    first = tuple(
+        pltpu.VMEM((2, 2, rows, w // 2) if relayed else (3, rows, w), bf16) for w, relayed in chunks
+    )
+    second = tuple(pltpu.VMEM((2, rows, w // 2), bf16) for w, _ in chunks)
+    many = len(chunks)
+    return [
+        pltpu.VMEM((tokens, slab), bf16),
+        pltpu.VMEM((slab, tokens), bf16),
+        tuple(pltpu.VMEM((tokens, w), bf16) for w, _ in chunks),
+        state, state, state, state,
+        stage, paired, first, first, second, second,
+        pltpu.VMEM((n * depth, 1, 128), f32),
+        dma((PARTS,)), dma((many,)), dma((3,)),
+        dma, dma((many,)),
+        dma((many,)), dma((many, 3)),
+        dma((many,)), dma((many, 2)),
+        dma, dma,
+        dma((2,)), dma((len(PIECES), 3)),
+        dma, dma((len(PIECES), 2)),
+        dma, dma,
+    ]
+
+
+def square_kernel(
+    n, depth,
+    hid, lgr, mas, one, two,
+    rows_out, mas_out, one_out, two_out,
+    lgr_v, lgt_v, hid_v, mas_v, one_v, two_v, grad,
+    stage, paired, p1_out, p1_in, p2_out, p2_in, sq_all,
+    lgr_sem, hid_sem, state_sem, pair_send, pair_recv, p1_send, p1_recv, p2_send, p2_recv,
+    sq_send, sq_recv, ag_send, ag_recv, far_send, far_recv, relay_send, relay_recv,
+):
+    total = n * depth
+    rows, width = grad.shape
+    f32, bf16 = jnp.float32, jnp.bfloat16
+    dp, fs = lax.axis_index("dp"), lax.axis_index("fsdp")
+    chip, core = dp // 2, dp % 2
+    other = 1 - core
+    x, y = chip % 2, chip // 2
+    near = (2 * y + 1 - x, 2 * (1 - y) + x)
+    far = 2 * (1 - y) + 1 - x
+    me = dp * depth + fs
+    partner = (2 * chip + other, fs)
+    across = tuple((2 * q + core, fs) for q in near + (far,))
+    chunks, pieces_ = spans(width, CHUNKS), spans(width, PIECES)
+    steps = sorted(
+        ((z, b, a, c) for z in range(depth) for b in range(2) for a in range(2) for c in range(2)),
+        key=lambda s: -(min(s[0], depth - s[0]) + s[1] + s[2] + s[3] / 4),
+    )[:-1]
+
+    def each_other_device(act):
+        for dz, b, a, c in steps:
+            to_y = 1 - y if b else y
+            to_x = 1 - x if a else x
+            to_core = other if c else core
+            act(((2 * to_y + to_x) * 2 + to_core, (fs + dz) % depth))
+
+    def remote(src, dst, send, recv, to):
+        return pltpu.make_async_remote_copy(
+            src_ref=src, dst_ref=dst, send_sem=send, recv_sem=recv, device_id=to, device_id_type=MESH
+        )
+
+    def settle(ref, sem):
+        pltpu.make_async_copy(ref, ref, sem).wait()
+
+    step = lgr.shape[0] // PARTS
+    lgr_loads = [
+        pltpu.make_async_copy(lgr.at[pl.ds(i * step, step)], lgr_v.at[pl.ds(i * step, step)], lgr_sem.at[i])
+        for i in range(PARTS)
+    ]
+    for load in lgr_loads:
+        load.start()
+    loads = [
+        pltpu.make_async_copy(hid.at[:, pl.ds(start, w)], hid_v[j], hid_sem.at[j])
+        for j, (start, w, _) in enumerate(chunks)
+    ]
+    for load in loads[:AHEAD]:
+        load.start(priority=1)
+    barrier = pltpu.get_barrier_semaphore()
+    each_other_device(
+        lambda to: pl.semaphore_signal(barrier, inc=1, device_id=to, device_id_type=MESH)
+    )
+    states = [
+        pltpu.make_async_copy(src, dst, state_sem.at[i])
+        for i, (src, dst) in enumerate(((mas, mas_v), (one, one_v), (two, two_v)))
+    ]
+
+    def pair_copy(j):
+        return remote(stage[j].at[other], paired[j], pair_send, pair_recv.at[j], partner)
+
+    def first_copy(j, way):
+        return remote(p1_out[j].at[way], p1_in[j].at[way], p1_send.at[j], p1_recv.at[j, way], across[way])
+
+    def second_copy(j, way):
+        return remote(p2_out[j].at[way], p2_in[j].at[way], p2_send.at[j], p2_recv.at[j, way], across[way])
+
+    def both(j, q, start, w):
+        cols = pl.ds(start, w)
+        return stage[j][core, q, :, cols].astype(f32) + paired[j][q, :, cols].astype(f32)
+
+    def chip_sum(j):
+        start, w, relayed = chunks[j]
+        wh = w // 2
+        pair_copy(j).wait_recv()
+        if relayed:
+            for way in range(2):
+                p1_out[j][way, 1] = both(j, far, way * wh, wh).astype(bf16)
+                p1_out[j][way, 0] = both(j, near[way], way * wh, wh).astype(bf16)
+                first_copy(j, way).start()
+        else:
+            for way, q in ((2, far), (0, near[0]), (1, near[1])):
+                p1_out[j][way] = both(j, q, 0, w).astype(bf16)
+                first_copy(j, way).start()
+        grad[:, pl.ds(start, w)] = both(j, chip, 0, w)
+
+    for i in range(PARTS):
+        lgr_loads[i].wait()
+        lgt_v[:, i * step : (i + 1) * step] = lgr_v[i * step : (i + 1) * step, :].T
+    for j in range(len(chunks)):
+        loads[j].wait()
+        if j + AHEAD < len(chunks):
+            loads[j + AHEAD].start(priority=1)
+        part = jnp.dot(lgt_v[...], hid_v[j][...], preferred_element_type=f32).astype(bf16)
+        for q in range(n // 2):
+            for c in range(2):
+                d = 2 * q + c
+                stage[j][c, q] = part[d * rows : (d + 1) * rows, :]
+        if j == 0:
+            pl.semaphore_wait(barrier, total - 1)
+        pair_copy(j).start()
+        if j > 0:
+            chip_sum(j - 1)
+    for load in states:
+        load.start()
+    chip_sum(len(chunks) - 1)
+
+    relayed_chunks = [j for j in range(len(chunks)) if chunks[j][2]]
+    for j in relayed_chunks:
+        wh = chunks[j][1] // 2
+        for way in range(2):
+            first_copy(j, way).wait_recv()
+            away = 1 - way
+            joined = both(j, near[away], way * wh, wh) + p1_in[j][way, 1].astype(f32)
+            p2_out[j][away] = joined.astype(bf16)
+            second_copy(j, away).start()
+
+    squares = jnp.zeros((8, 128), f32)
+
+    def add(start, w, terms, squares):
+        span = pl.ds(start, w)
+        value = grad[:, span]
+        for term in terms:
+            value = value + term.astype(f32)
+        grad[:, span] = value
+        value = value * value
+        for r in range(rows // 8):
+            for s in range(w // 128):
+                squares = squares + value[r * 8 : (r + 1) * 8, s * 128 : (s + 1) * 128]
+        return squares
+
+    for j in relayed_chunks:
+        start, w, _ = chunks[j]
+        wh = w // 2
+        for way in range(2):
+            second_copy(j, 1 - way).wait_recv()
+            squares = add(start + way * wh, wh, (p1_in[j][way, 0], p2_in[j][1 - way]), squares)
+    for j, (start, w, relayed) in enumerate(chunks):
+        if not relayed:
+            for way in range(3):
+                first_copy(j, way).wait_recv()
+            squares = add(start, w, [p1_in[j][way] for way in range(3)], squares)
+
+    sq_all[me] = jnp.sum(squares, axis=0, keepdims=True)
+    each_other_device(
+        lambda to: remote(sq_all.at[me], sq_all.at[me], sq_send, sq_recv, to).start()
+    )
+    for load in states:
+        load.wait()
+    everyone = sq_all.at[pl.ds(0, total - 1)]
+    settle(everyone, sq_recv)
+    sumsq = jnp.sum(jnp.sum(sq_all[...], axis=0), axis=1, keepdims=True)
+    rms = jnp.sqrt(sumsq / (rows * n * width * depth))
+    factor = jnp.where(rms > 1.0, 1.0 / rms, 1.0)
+
+    def block(q, start, w):
+        return rows_out.at[pl.ds(pl.multiple_of((2 * q + core) * rows, rows), rows), pl.ds(start, w)]
+
+    def own_copy(k, way, q):
+        start, w, relayed = pieces_[k]
+        sem = ag_send.at[0 if relayed else 1]
+        return remote(block(q, start, w), block(q, start, w), sem, ag_recv.at[k, way], across[way])
+
+    def far_copy(k, way, q):
+        start, w, _ = pieces_[k]
+        part = block(q, start + way * (w // 2), w // 2)
+        return remote(part, part, far_send, far_recv.at[k, way], across[1 - way])
+
+    def relay(q, start, w):
+        return remote(block(q, start, w), block(q, start, w), relay_send, relay_recv, partner)
+
+    for k, (start, w, relayed) in enumerate(pieces_):
+        span = pl.ds(start, w)
+        clipped = factor * grad[:, span]
+        new_one = 0.9 * one_v[:, span] + 0.1 * clipped
+        new_two = 0.95 * two_v[:, span] + 0.05 * clipped * clipped
+        first = new_one / (1.0 - 0.9**10)
+        second = new_two / (1.0 - 0.95**10)
+        held = mas_v[:, span]
+        new_master = held - 0.05 * (first / (jnp.sqrt(second) + 1e-08) + 0.1 * held)
+        rows_out[pl.ds(pl.multiple_of(dp * rows, rows), rows), span] = new_master.astype(bf16)
+        for way in (0, 1) if relayed else (2, 0, 1):
+            own_copy(k, way, chip).start()
+        relay(chip, start, w).start()
+        one_out[:, span] = new_one
+        two_out[:, span] = new_two
+        mas_out[:, span] = new_master
+
+    for k, (start, w, relayed) in enumerate(pieces_):
+        if relayed:
+            for way in range(2):
+                own_copy(k, way, near[way]).wait_recv()
+                far_copy(k, way, near[way]).start()
+                relay(near[way], start, w).start()
+    for k, (start, w, relayed) in enumerate(pieces_):
+        if not relayed:
+            for way, q in ((0, near[0]), (1, near[1]), (2, far)):
+                own_copy(k, way, q).wait_recv()
+                relay(q, start, w).start()
+    for k, (start, w, relayed) in enumerate(pieces_):
+        if relayed:
+            for way in range(2):
+                far_copy(k, way, far).wait_recv()
+                relay(far, start + way * (w // 2), w // 2).start()
+
+    for j, (_, w, relayed) in enumerate(chunks):
+        settle(paired[j], pair_send)
+        settle(p1_in[j], p1_send.at[j])
+        if relayed:
+            settle(p2_in[j], p2_send.at[j])
+    settle(everyone, sq_send)
+    sent = sum(w for _, w, relayed in pieces_ if relayed)
+    settle(rows_out.at[pl.ds(0, 2 * rows), pl.ds(0, sent)], ag_send.at[0])
+    settle(rows_out.at[pl.ds(0, rows), pl.ds(0, sent)], far_send)
+    if sent < width:
+        settle(rows_out.at[pl.ds(0, 3 * rows), pl.ds(0, width - sent)], ag_send.at[1])
+    settle(rows_out.at[pl.ds(0, 4 * rows)], relay_send)
+    settle(rows_out.at[pl.ds(0, 4 * rows)], relay_recv)
+
+
 def write_out(*refs):
     sems = refs[8]
     copies = [pltpu.make_async_copy(refs[i], refs[4 + i], sems.at[i]) for i in range(4)]
@@ -202,9 +471,6 @@
     slab = logit_grad.shape[1]
     rows = master.shape[0]
     chips = n // 2
-    chunks = pieces(width, LOAD_CHUNKS)
-    gathers = pieces(width, GATHER_CHUNKS)
-    wc = width // chunks
     f32, bf16 = jnp.float32, jnp.bfloat16
     state = ((rows, width), f32)
     shapes = (((slab, width), bf16), state, state, state)
@@ -212,12 +478,15 @@
     dma = pltpu.SemaphoreType.DMA
     anywhere = pl.BlockSpec(memory_space=pl.ANY)
     in_vmem = pl.BlockSpec(memory_space=pltpu.VMEM)
-    held = pl.pallas_call(
-        functools.partial(kernel, n, depth, chunks, gathers),
-        out_shape=tuple(pltpu.VMEM(*shape) for shape in shapes),
-        in_specs=[anywhere] * 5,
-        out_specs=(in_vmem,) * 4,
-        scratch_shapes=[
+    if n == 8 and width % (UNITS * 256) == 0 and tokens % (PARTS * 128) == 0:
+        body = functools.partial(square_kernel, n, depth)
+        scratch = square_scratch(n, depth, tokens, slab, rows, width)
+    else:
+        chunks = pieces(width, LOAD_CHUNKS)
+        gathers = pieces(width, GATHER_CHUNKS)
+        wc = width // chunks
+        body = functools.partial(direct_kernel, n, depth, chunks, gathers)
+        scratch = [
             pltpu.VMEM((tokens, slab), bf16),
             pltpu.VMEM((slab, tokens), bf16),
             pltpu.VMEM((chunks, tokens, wc), bf16),
@@ -243,7 +512,13 @@
             dma((gathers, chips)),
             dma((gathers, chips)),
             dma((gathers, chips)),
-        ],
+        ]
+    held = pl.pallas_call(
+        body,
+        out_shape=tuple(pltpu.VMEM(*shape) for shape in shapes),
+        in_specs=[anywhere] * 5,
+        out_specs=(in_vmem,) * 4,
+        scratch_shapes=scratch,
         compiler_params=pltpu.CompilerParams(
             collective_id=0, has_side_effects=True, vmem_limit_bytes=VMEM_BYTES - kept - 96 * 1024
         ),

time: 33.3 us -> 30.6 us (0.919)
  Pallas kernels: 32.5 us -> 29.8 us
    pallas_call x1, Pallas kernels: 31.2 us -> 28.6 us  [shards(): pl.pallas_call(body, out_shape=tuple((pltpu.VMEM(*shape) for shape in sha...]
where the time goes in v1:
time: 30.6 us; the launch traced here: 30.5 us
  Pallas kernels  29.8 us (97%)
  between operations  0.64 us (2%)
    pallas_call x1, Pallas kernels, shards(): pl.pallas_call(body, out_shape=tuple((pltpu.VMEM(*shape) for shape in sha...  28.6 us
    pallas_call x1, Pallas kernels, shards(): pl.pallas_call(write_out, out_shape=tuple((pltpu.HBM(*shape) for shape in...  1.26 us

profile of v1, /device:TPU:0, one launch (start us, length us, event | category | flops | bytes accessed | tf_op | source)
XLA Modules:
  0.0 30.5 jit_solution(17479575386763402786)
XLA Ops:
  0.6 28.6 %shard_map.84 = (bf16[256,2048]{1,0:T(8,128)(2,1)S(1)}, f32[32,2048]{1,0:T(8,128)S(1)}, f32[32,2048]{1,0:T(8,128)S(1)}, f32[32,2048]{1,0:T(8,128)S(1)}) custom-call(bf16[2048,2048]{1,0:T(8,128)(2,1)} %hid.1, bf16[2048,256]{1,0:T(8,128)(2,1)} %lgr.1, f32[32,2048]{1,0:T(8,128)} %mas.1, f32[32,2048]{1,0:T(8,128)} %one.1, f32[32,2048]{1,0:T(8,128)} %two.1), custom_call_target="tpu_custom_call" | custom-call | tf_op jit(solution)/shard_map/pallas_call | solution.py:516
  29.2 1.3 %shard_map.85 = (bf16[256,2048]{1,0:T(8,128)(2,1)}, f32[32,2048]{1,0:T(8,128)}, f32[32,2048]{1,0:T(8,128)}, f32[32,2048]{1,0:T(8,128)}) custom-call(bf16[256,2048]{1,0:T(8,128)(2,1)S(1)} %get-tuple-element.8.refs_0_, f32[32,2048]{1,0:T(8,128)S(1)} %get-tuple-element.9.refs_1_, f32[32,2048]{1,0:T(8,128)S(1)} %get-tuple-element.10.refs_2_, ...), custom_call_target="tpu_custom_call" | custom-call | tf_op jit(solution)/shard_map/pallas_call | solution.py:526

commit v2 on v1

--- a/solution.py
+++ b/solution.py
@@ -13,8 +13,10 @@
 VMEM_BYTES = 67_043_328
 UNITS = 8
 PARTS = 4
-CHUNKS = ((1, False), (2, False), (2, False), (2, False), (1, False))
-PIECES = ((2, True), (2, False), (2, False), (2, False))
+CHUNKS = ((1, False), (2, False), (2, False), (3, False))
+PIECES = ((2, True), (2, False), (3, False))
+KITS = 1
+EARLY = 0
 AHEAD = 2
 
 
@@ -219,6 +221,7 @@
         tuple(pltpu.VMEM((tokens, w), bf16) for w, _ in chunks),
         state, state, state, state,
         stage, paired, first, first, second, second,
+        tuple(pltpu.VMEM((4, 4, rows, width // UNITS), bf16) for _ in range(KITS)),
         pltpu.VMEM((n * depth, 1, 128), f32),
         dma((PARTS,)), dma((many,)), dma((3,)),
         dma, dma((many,)),
@@ -228,6 +231,7 @@
         dma((2,)), dma((len(PIECES), 3)),
         dma, dma((len(PIECES), 2)),
         dma, dma,
+        dma((KITS,)), dma((KITS, 2, 3)),
     ]
 
 
@@ -236,9 +240,10 @@
     hid, lgr, mas, one, two,
     rows_out, mas_out, one_out, two_out,
     lgr_v, lgt_v, hid_v, mas_v, one_v, two_v, grad,
-    stage, paired, p1_out, p1_in, p2_out, p2_in, sq_all,
+    stage, paired, p1_out, p1_in, p2_out, p2_in, kit, sq_all,
     lgr_sem, hid_sem, state_sem, pair_send, pair_recv, p1_send, p1_recv, p2_send, p2_recv,
     sq_send, sq_recv, ag_send, ag_recv, far_send, far_recv, relay_send, relay_recv,
+    kit_send, kit_recv,
 ):
     total = n * depth
     rows, width = grad.shape
@@ -253,6 +258,8 @@
     partner = (2 * chip + other, fs)
     across = tuple((2 * q + core, fs) for q in near + (far,))
     chunks, pieces_ = spans(width, CHUNKS), spans(width, PIECES)
+    unit = width // UNITS
+    kits = [width - (KITS - p) * unit for p in range(KITS)]
     steps = sorted(
         ((z, b, a, c) for z in range(depth) for b in range(2) for a in range(2) for c in range(2)),
         key=lambda s: -(min(s[0], depth - s[0]) + s[1] + s[2] + s[3] / 4),
@@ -284,8 +291,7 @@
         pltpu.make_async_copy(hid.at[:, pl.ds(start, w)], hid_v[j], hid_sem.at[j])
         for j, (start, w, _) in enumerate(chunks)
     ]
-    for load in loads[:AHEAD]:
-        load.start(priority=1)
+    loads[0].start(priority=1)
     barrier = pltpu.get_barrier_semaphore()
     each_other_device(
         lambda to: pl.semaphore_signal(barrier, inc=1, device_id=to, device_id_type=MESH)
@@ -323,13 +329,19 @@
                 first_copy(j, way).start()
         grad[:, pl.ds(start, w)] = both(j, chip, 0, w)
 
+    loads[1].start(priority=1)
     for i in range(PARTS):
         lgr_loads[i].wait()
         lgt_v[:, i * step : (i + 1) * step] = lgr_v[i * step : (i + 1) * step, :].T
+    for load in loads[2:AHEAD]:
+        load.start(priority=1)
     for j in range(len(chunks)):
         loads[j].wait()
         if j + AHEAD < len(chunks):
             loads[j + AHEAD].start(priority=1)
+        elif j + AHEAD == len(chunks):
+            for load in states:
+                load.start()
         part = jnp.dot(lgt_v[...], hid_v[j][...], preferred_element_type=f32).astype(bf16)
         for q in range(n // 2):
             for c in range(2):
@@ -340,9 +352,28 @@
         pair_copy(j).start()
         if j > 0:
             chip_sum(j - 1)
+    chip_sum(len(chunks) - 1)
+
+    def state_copy(p, way):
+        return remote(
+            kit[p].at[3, pl.ds(0, 3)], kit[p].at[way, pl.ds(0, 3)], kit_send.at[p], kit_recv.at[p, 0, way], across[way]
+        )
+
+    def grad_copy(p, way):
+        return remote(kit[p].at[3, 3], kit[p].at[way, 3], kit_send.at[p], kit_recv.at[p, 1, way], across[way])
+
+    correct_one, correct_two = 1.0 - 0.9**10, 1.0 - 0.95**10
     for load in states:
-        load.start()
-    chip_sum(len(chunks) - 1)
+        load.wait()
+    for p, start in enumerate(kits):
+        span = pl.ds(start, unit)
+        held = mas_v[:, span]
+        kit[p][3, 0] = (held - 0.05 * 0.1 * held).astype(bf16)
+        kit[p][3, 1] = (0.05 * 0.9 / correct_one * one_v[:, span]).astype(bf16)
+        kit[p][3, 2] = (0.95 / correct_two * two_v[:, span]).astype(bf16)
+        if p < EARLY:
+            for way in (2, 0, 1):
+                state_copy(p, way).start()
 
     relayed_chunks = [j for j in range(len(chunks)) if chunks[j][2]]
     for j in relayed_chunks:
@@ -384,8 +415,16 @@
     each_other_device(
         lambda to: remote(sq_all.at[me], sq_all.at[me], sq_send, sq_recv, to).start()
     )
-    for load in states:
-        load.wait()
+    for p, start in enumerate(kits):
+        kit[p][3, 3] = grad[:, pl.ds(start, unit)].astype(bf16)
+        if p < EARLY:
+            for way in (2, 0, 1):
+                grad_copy(p, way).start()
+    for p in range(EARLY, KITS):
+        for way in (2, 0, 1):
+            state_copy(p, way).start()
+        for way in (2, 0, 1):
+            grad_copy(p, way).start()
     everyone = sq_all.at[pl.ds(0, total - 1)]
     settle(everyone, sq_recv)
     sumsq = jnp.sum(jnp.sum(sq_all[...], axis=0), axis=1, keepdims=True)
@@ -408,22 +447,41 @@
     def relay(q, start, w):
         return remote(block(q, start, w), block(q, start, w), relay_send, relay_recv, partner)
 
-    for k, (start, w, relayed) in enumerate(pieces_):
+    def update(start, w):
         span = pl.ds(start, w)
         clipped = factor * grad[:, span]
         new_one = 0.9 * one_v[:, span] + 0.1 * clipped
         new_two = 0.95 * two_v[:, span] + 0.05 * clipped * clipped
-        first = new_one / (1.0 - 0.9**10)
-        second = new_two / (1.0 - 0.95**10)
+        first = new_one / correct_one
+        second = new_two / correct_two
         held = mas_v[:, span]
         new_master = held - 0.05 * (first / (jnp.sqrt(second) + 1e-08) + 0.1 * held)
-        rows_out[pl.ds(pl.multiple_of(dp * rows, rows), rows), span] = new_master.astype(bf16)
+        one_out[:, span] = new_one
+        two_out[:, span] = new_two
+        mas_out[:, span] = new_master
+        return new_master
+
+    def rows_of(d):
+        return pl.ds(pl.multiple_of(d * rows, rows), rows)
+
+    for k, (start, w, relayed) in enumerate(pieces_):
+        rows_out[rows_of(dp), pl.ds(start, w)] = update(start, w).astype(bf16)
         for way in (0, 1) if relayed else (2, 0, 1):
             own_copy(k, way, chip).start()
         relay(chip, start, w).start()
-        one_out[:, span] = new_one
-        two_out[:, span] = new_two
-        mas_out[:, span] = new_master
+    for p, start in enumerate(kits):
+        update(start, unit)
+        for way in range(3):
+            state_copy(p, way).wait_recv()
+            grad_copy(p, way).wait_recv()
+        for slot, q in enumerate(near + (far, chip)):
+            base, step_one, step_two, part = (kit[p][slot, i].astype(f32) for i in range(4))
+            clipped = factor * part
+            step_one = step_one + 0.05 * 0.1 / correct_one * clipped
+            step_two = step_two + 0.05 / correct_two * clipped * clipped
+            new_rows = base - step_one / (jnp.sqrt(step_two) + 1e-08)
+            rows_out[rows_of(2 * q + core), pl.ds(start, unit)] = new_rows.astype(bf16)
+            relay(q, start, unit).start()
 
     for k, (start, w, relayed) in enumerate(pieces_):
         if relayed:
@@ -451,8 +509,11 @@
     sent = sum(w for _, w, relayed in pieces_ if relayed)
     settle(rows_out.at[pl.ds(0, 2 * rows), pl.ds(0, sent)], ag_send.at[0])
     settle(rows_out.at[pl.ds(0, rows), pl.ds(0, sent)], far_send)
-    if sent < width:
-        settle(rows_out.at[pl.ds(0, 3 * rows), pl.ds(0, width - sent)], ag_send.at[1])
+    straight = width - KITS * unit - sent
+    if straight > 0:
+        settle(rows_out.at[pl.ds(0, 3 * rows), pl.ds(0, straight)], ag_send.at[1])
+    for p in range(KITS):
+        settle(kit[p].at[pl.ds(0, 3)], kit_send.at[p])
     settle(rows_out.at[pl.ds(0, 4 * rows)], relay_send)
     settle(rows_out.at[pl.ds(0, 4 * rows)], relay_recv)
 

time: 30.6 us -> 29.8 us (0.974)
  Pallas kernels: 29.8 us -> 29 us
    pallas_call x1, Pallas kernels: 28.6 us -> 27.8 us  [shards(): pl.pallas_call(body, out_shape=tuple((pltpu.VMEM(*shape) for shape in sha...]
where the time goes in v2:
time: 29.8 us; the launch traced here: 29.7 us
  Pallas kernels  29 us (97%)
  between operations  0.64 us (2%)
    pallas_call x1, Pallas kernels, shards(): pl.pallas_call(body, out_shape=tuple((pltpu.VMEM(*shape) for shape in sha...  27.8 us
    pallas_call x1, Pallas kernels, shards(): pl.pallas_call(write_out, out_shape=tuple((pltpu.HBM(*shape) for shape in...  1.26 us

profile of v2, /device:TPU:0, one launch (start us, length us, event | category | flops | bytes accessed | tf_op | source)
XLA Modules:
  0.0 29.7 jit_solution(5297172641948865257)
XLA Ops:
  0.6 27.8 %shard_map.84 = (bf16[256,2048]{1,0:T(8,128)(2,1)S(1)}, f32[32,2048]{1,0:T(8,128)S(1)}, f32[32,2048]{1,0:T(8,128)S(1)}, f32[32,2048]{1,0:T(8,128)S(1)}) custom-call(bf16[2048,2048]{1,0:T(8,128)(2,1)} %hid.1, bf16[2048,256]{1,0:T(8,128)(2,1)} %lgr.1, f32[32,2048]{1,0:T(8,128)} %mas.1, f32[32,2048]{1,0:T(8,128)} %one.1, f32[32,2048]{1,0:T(8,128)} %two.1), custom_call_target="tpu_custom_call" | custom-call | tf_op jit(solution)/shard_map/pallas_call | solution.py:577
  28.4 1.3 %shard_map.85 = (bf16[256,2048]{1,0:T(8,128)(2,1)}, f32[32,2048]{1,0:T(8,128)}, f32[32,2048]{1,0:T(8,128)}, f32[32,2048]{1,0:T(8,128)}) custom-call(bf16[256,2048]{1,0:T(8,128)(2,1)S(1)} %get-tuple-element.8.refs_0_, f32[32,2048]{1,0:T(8,128)S(1)} %get-tuple-element.9.refs_1_, f32[32,2048]{1,0:T(8,128)S(1)} %get-tuple-element.10.refs_2_, ...), custom_call_target="tpu_custom_call" | custom-call | tf_op jit(solution)/shard_map/pallas_call | solution.py:587

commit v3 on v2

--- a/solution.py
+++ b/solution.py
@@ -13,8 +13,8 @@
 VMEM_BYTES = 67_043_328
 UNITS = 8
 PARTS = 4
-CHUNKS = ((1, False), (2, False), (2, False), (3, False))
-PIECES = ((2, True), (2, False), (3, False))
+CHUNKS = ((2, True), (2, True), (2, False), (2, False))
+PIECES = ((2, True), (3, False), (2, False))
 KITS = 1
 EARLY = 0
 AHEAD = 2
@@ -412,9 +412,18 @@
             squares = add(start, w, [p1_in[j][way] for way in range(3)], squares)
 
     sq_all[me] = jnp.sum(squares, axis=0, keepdims=True)
-    each_other_device(
-        lambda to: remote(sq_all.at[me], sq_all.at[me], sq_send, sq_recv, to).start()
-    )
+    def tell(to_y, to_x, to_core, to_z):
+        to = ((2 * to_y + to_x) * 2 + to_core, to_z)
+        remote(sq_all.at[me], sq_all.at[me], sq_send, sq_recv, to).start()
+
+    for to_z in range(depth):
+        for to_y, to_x, to_core in (
+            (1 - y, 1 - x, other), (1 - y, 1 - x, core), (1 - y, x, other), (y, 1 - x, other),
+            (1 - y, x, core), (y, 1 - x, core), (y, x, other),
+        ):
+            tell(to_y, to_x, to_core, to_z)
+    for dz in range(1, depth):
+        tell(y, x, core, (fs + dz) % depth)
     for p, start in enumerate(kits):
         kit[p][3, 3] = grad[:, pl.ds(start, unit)].astype(bf16)
         if p < EARLY:

time: 29.8 us -> 29.7 us (level)
  no operation moved by 1% of the time
where the time goes in v3:
time: 29.7 us; the launch traced here: 29.5 us
  Pallas kernels  28.9 us (97%)
  between operations  0.64 us (2%)
    pallas_call x1, Pallas kernels, shards(): pl.pallas_call(body, out_shape=tuple((pltpu.VMEM(*shape) for shape in sha...  27.6 us
    pallas_call x1, Pallas kernels, shards(): pl.pallas_call(write_out, out_shape=tuple((pltpu.HBM(*shape) for shape in...  1.26 us

profile of v3, /device:TPU:0, one launch (start us, length us, event | category | flops | bytes accessed | tf_op | source)
XLA Modules:
  0.0 29.5 jit_solution(1822764484864704683)
XLA Ops:
  0.6 27.6 %shard_map.84 = (bf16[256,2048]{1,0:T(8,128)(2,1)S(1)}, f32[32,2048]{1,0:T(8,128)S(1)}, f32[32,2048]{1,0:T(8,128)S(1)}, f32[32,2048]{1,0:T(8,128)S(1)}) custom-call(bf16[2048,2048]{1,0:T(8,128)(2,1)} %hid.1, bf16[2048,256]{1,0:T(8,128)(2,1)} %lgr.1, f32[32,2048]{1,0:T(8,128)} %mas.1, f32[32,2048]{1,0:T(8,128)} %one.1, f32[32,2048]{1,0:T(8,128)} %two.1), custom_call_target="tpu_custom_call" | custom-call | tf_op jit(solution)/shard_map/pallas_call | solution.py:586
  28.3 1.3 %shard_map.85 = (bf16[256,2048]{1,0:T(8,128)(2,1)}, f32[32,2048]{1,0:T(8,128)}, f32[32,2048]{1,0:T(8,128)}, f32[32,2048]{1,0:T(8,128)}) custom-call(bf16[256,2048]{1,0:T(8,128)(2,1)S(1)} %get-tuple-element.8.refs_0_, f32[32,2048]{1,0:T(8,128)S(1)} %get-tuple-element.9.refs_1_, f32[32,2048]{1,0:T(8,128)S(1)} %get-tuple-element.10.refs_2_, ...), custom_call_target="tpu_custom_call" | custom-call | tf_op jit(solution)/shard_map/pallas_call | solution.py:596

commit v4 on v3

--- a/solution.py
+++ b/solution.py
@@ -478,6 +478,12 @@
         for way in (0, 1) if relayed else (2, 0, 1):
             own_copy(k, way, chip).start()
         relay(chip, start, w).start()
+    for k, (start, w, relayed) in enumerate(pieces_):
+        if relayed:
+            for way in range(2):
+                own_copy(k, way, near[way]).wait_recv()
+                far_copy(k, way, near[way]).start()
+                relay(near[way], start, w).start()
     for p, start in enumerate(kits):
         update(start, unit)
         for way in range(3):
@@ -492,12 +498,6 @@
             rows_out[rows_of(2 * q + core), pl.ds(start, unit)] = new_rows.astype(bf16)
             relay(q, start, unit).start()
 
-    for k, (start, w, relayed) in enumerate(pieces_):
-        if relayed:
-            for way in range(2):
-                own_copy(k, way, near[way]).wait_recv()
-                far_copy(k, way, near[way]).start()
-                relay(near[way], start, w).start()
     for k, (start, w, relayed) in enumerate(pieces_):
         if not relayed:
             for way, q in ((0, near[0]), (1, near[1]), (2, far)):

time: 29.7 us -> 29.7 us (level)
  no operation moved by 1% of the time
where the time goes in v4:
time: 29.7 us; the launch traced here: 29.5 us
  Pallas kernels  28.9 us (97%)
  between operations  0.64 us (2%)
    pallas_call x1, Pallas kernels, shards(): pl.pallas_call(body, out_shape=tuple((pltpu.VMEM(*shape) for shape in sha...  27.6 us
    pallas_call x1, Pallas kernels, shards(): pl.pallas_call(write_out, out_shape=tuple((pltpu.HBM(*shape) for shape in...  1.26 us

profile of v4, /device:TPU:0, one launch (start us, length us, event | category | flops | bytes accessed | tf_op | source)
XLA Modules:
  0.0 29.5 jit_solution(13991429245016324350)
XLA Ops:
  0.6 27.6 %shard_map.84 = (bf16[256,2048]{1,0:T(8,128)(2,1)S(1)}, f32[32,2048]{1,0:T(8,128)S(1)}, f32[32,2048]{1,0:T(8,128)S(1)}, f32[32,2048]{1,0:T(8,128)S(1)}) custom-call(bf16[2048,2048]{1,0:T(8,128)(2,1)} %hid.1, bf16[2048,256]{1,0:T(8,128)(2,1)} %lgr.1, f32[32,2048]{1,0:T(8,128)} %mas.1, f32[32,2048]{1,0:T(8,128)} %one.1, f32[32,2048]{1,0:T(8,128)} %two.1), custom_call_target="tpu_custom_call" | custom-call | tf_op jit(solution)/shard_map/pallas_call | solution.py:586
  28.3 1.3 %shard_map.85 = (bf16[256,2048]{1,0:T(8,128)(2,1)}, f32[32,2048]{1,0:T(8,128)}, f32[32,2048]{1,0:T(8,128)}, f32[32,2048]{1,0:T(8,128)}) custom-call(bf16[256,2048]{1,0:T(8,128)(2,1)S(1)} %get-tuple-element.8.refs_0_, f32[32,2048]{1,0:T(8,128)S(1)} %get-tuple-element.9.refs_1_, f32[32,2048]{1,0:T(8,128)S(1)} %get-tuple-element.10.refs_2_, ...), custom_call_target="tpu_custom_call" | custom-call | tf_op jit(solution)/shard_map/pallas_call | solution.py:596
